TPU v7x, 32 devices: a whole 2x2x4 slice. The times are simulated.
32 devices in a mesh: dp: 16 (over z, y, x), sub: 2 (over core).
Axes of the slice: x: 2, y: 2, z: 4, core: 2. Of those that a mesh axis runs over, the one named last changes fastest.
Arguments:
- projections: float32 [6144, 128], P(('dp', 'sub')), may hold values from -6 to 6
- partner: int32 [6144], P(('dp', 'sub')), may hold values from 0 to 6143, as said below
Outputs:
- loss: float32 [], replicated
- grad_projections: float32 [6144, 128], P(('dp', 'sub'))
Inputs may be any that keep to these rules, and one draw needn't show every extreme that they name: partner pairs the views: partner[partner[i]] = i and partner[i] != i for every view.
All inputs are finite; a program needn't handle non-finite values.
Results may differ from a plain program's by a relative error of at most 0.0003.
The roundings to bfloat16 on the way count: a program that leaves them out, or rounds other values in their place, can miss the bound.
Values may be sent and summed in bfloat16 or wider, within the bound.
A program may use at most 128 MiB of HBM per device.

v0:
```python
import jax
import jax.numpy as jnp
from jax import lax
from jax.sharding import PartitionSpec as P

TAU = 0.1
SHIFT = 10.0


def tile_scores(left_low, piece):
    return (
        lax.dot_general(
            left_low, piece, (((1,), (1,)), ((), ())), preferred_element_type=jnp.float32
        )
        / TAU
    )


def make_forward(left_low, row_ids, mates, column_ids):

    def forward_step(carry, piece, start):
        score = tile_scores(left_low, piece)
        cols = column_ids(start, piece.shape[0])
        diag = cols[None, :] == row_ids[:, None]
        hit = cols[None, :] == mates[:, None]
        total = jnp.sum(jnp.where(diag, 0.0, jnp.exp(score - SHIFT)), axis=1)
        pos = jnp.sum(jnp.where(hit, score, 0.0), axis=1)
        return (total, pos)

    return forward_step


def make_backward(left_low, row_ids, mates, column_ids, lse_rows, lse_cols):

    def backward_step(carry, piece, start):
        score = tile_scores(left_low, piece)
        count = piece.shape[0]
        cols = column_ids(start, count)
        diag = cols[None, :] == row_ids[:, None]
        hit = cols[None, :] == mates[:, None]
        weight = jnp.exp(score - lse_rows[:, None]) + jnp.exp(score - lse_cols[None, :])
        weight = weight - 2.0 * hit.astype(jnp.float32)
        weight = jnp.where(diag, 0.0, weight / TAU).astype(jnp.bfloat16)
        return jnp.dot(weight, piece, preferred_element_type=jnp.float32)

    return backward_step


def body(projections, partner):
    vrows = projections.shape[0]
    width_d = projections.shape[1]
    groups = lax.axis_size(("dp", "sub"))
    views_all = vrows * groups
    inverse = lax.rsqrt(jnp.sum(projections * projections, axis=1) + 1e-06)
    unit = projections * inverse[:, None]
    unit_low = unit.astype(jnp.bfloat16)
    rows = lax.axis_index(("dp", "sub")) * vrows + jnp.arange(vrows, dtype=jnp.int32)

    def plain_ids(start, count):
        return jnp.arange(count, dtype=jnp.int32)

    forward_step = make_forward(unit_low, rows, partner, plain_ids)
    empty = jnp.zeros((vrows,), jnp.float32)
    total, pos = forward_step(
        (empty, empty), lax.all_gather(unit_low, ("dp", "sub"), axis=0, tiled=True), jnp.int32(0)
    )
    lse = jnp.log(total) + SHIFT
    row_loss = lse - pos
    lse_all = lax.all_gather(lse, ("dp", "sub"), axis=0, tiled=True)
    loss = lax.psum(jnp.sum(row_loss), ("dp", "sub")) / views_all
    backward_step = make_backward(unit_low, rows, partner, plain_ids, lse, lse_all)
    start_grad = jnp.zeros((vrows, width_d), jnp.float32)
    grad_unit = backward_step(
        start_grad, lax.all_gather(unit_low, ("dp", "sub"), axis=0, tiled=True), jnp.int32(0)
    )
    inner = jnp.sum(unit * grad_unit, axis=1)
    grad = inverse[:, None] * (grad_unit - unit * inner[:, None])
    return (loss, grad)


def solution(mesh):
    return jax.shard_map(
        body,
        mesh=mesh,
        in_specs=(P(("dp", "sub"), None), P(("dp", "sub"))),
        out_specs=(P(), P(("dp", "sub"), None)),
        check_vma=False,
    )
```

profile of v0, /device:TPU:0, one launch (start us, length us, event | category | flops | bytes accessed | tf_op | source)
XLA Modules:
  0.0 129.2 jit_solution(13457414301605190832)
XLA Ops:
  7.2 0.0 all-gather.2.cloned.1.call-start
  7.2 1.0 multiply_reduce_fusion.1
  8.2 1.6 %multiply_convert_fusion = bf16[192,128]{1,0:T(8,128)(2,1)} fusion(f32[192,128]{1,0:T(8,128)} %param.2, f32[192]{0:T(256)S(1)} %add_rsqrt_fusion), kind=kLoop, calls=%fused_computation.10 | loop fusion | flops 49152 | bytes 148224 | tf_op jit(solution)/shard_map/convert_element_type | solution.py:56
  9.8 0.0 all-gather.2.cloned.1.call-update
  9.9 0.0 copy-start
  9.9 0.0 copy-start.2
  9.9 59.1 %all-gather.2.cloned.1.call-done = bf16[6144,128]{1,0:T(8,128)(2,1)} async-done(((bf16[192,128]{1,0:T(8,128)(2,1)}), bf16[6144,128]{1,0:T(8,128)(2,1)}) %all-gather.2.cloned.1.call-update) | async-done | bytes 1572880 | tf_op jit(solution)/shard_map/all_gather | solution.py:65
  69.0 0.0 copy-start.1
  69.0 5.7 %select_reduce_fusion.1 = (f32[192]{0:T(256)S(1)}, f32[192]{0:T(256)S(1)}, f32[192,6144]{1,0:T(8,128)}) fusion(s32[192]{0:T(256)S(1)} %iota_add_fusion, s32[192]{0:T(256)} %param.3, bf16[192,128]{1,0:T(8,128)(2,1)} %multiply_convert_fusion, bf16[6144,128]{1,0:T(8,128)(2,1)} %all-gather.2.cloned.1.call-done), kind=kOutput, calls=%fused_computation.4 | convolution fusion | flops 311426688 | bytes 6343680 | tf_op jit(solution)/shard_map/dot_general | solution.py:12
  74.7 0.7 log_add_fusion
  75.4 39.4 %all-reduce.1 = (f32[]{:T(128)}, f32[6144]{0:T(1024)S(1)}) all-reduce(f32[]{:T(128)} %get-tuple-element.7, f32[6144]{0:T(1024)S(1)} %get-tuple-element.8), channel_id=1, replica_groups=mesh['dp'=16,'sub'=2] {'dp','sub'}, use_global_device_ids=true, to_apply=%region_4.5 | all-reduce | flops 6145 | bytes 49160 | tf_op jit(solution)/shard_map/psum | solution.py:70
  115.5 0.0 copy-done
  115.5 0.0 copy-done.2
  115.5 0.0 copy-done.1
  115.5 5.0 %multiply_reduce_fusion = (f32[192]{0:T(256)S(1)}, f32[192,128]{1,0:T(8,128)S(1)}) fusion(f32[192,128]{1,0:T(8,128)S(1)} %copy-done, f32[192]{0:T(256)S(1)} %add_rsqrt_fusion, bf16[6144,128]{1,0:T(8,128)(2,1)S(1)} %copy-done.1, f32[192,6144]{1,0:T(8,128)} %get-tuple-element.9, f32[6144]{0:T(1024)S(1)} %get-tuple-element.5, f32[192]{0:T(256)S(1)} %get-tuple-element.6, ...), kind=kOutput, calls=%fused_computation.8 | convolution fusion | flops 313859904 | bytes 6516480 | tf_op jit(solution)/shard_map/dot_general | solution.py:44
  120.5 0.8 subtract_multiply_fusion
  (3 shorter events, 0.0 us)
Async XLA Ops:
  7.2 61.8 %all-gather.2.cloned.1.call-start = ((), (), s32[]{:S(2)}) async-start(), calls=%async_computation | async-start | bytes 1622016 | tf_op jit(solution)/shard_map/all_gather | solution.py:65
  9.9 105.6 %copy-start = (f32[192,128]{1,0:T(8,128)S(1)}, f32[192,128]{1,0:T(8,128)}, u32[]{:S(2)}) copy-start(f32[192,128]{1,0:T(8,128)} %param.2) | copy-start | bytes 294916
  9.9 105.6 %copy-start.2 = (s32[192]{0:T(256)S(1)}, s32[192]{0:T(256)}, u32[]{:S(2)}) copy-start(s32[192]{0:T(256)} %param.3) | copy-start | bytes 2308
  69.0 46.5 %copy-start.1 = (bf16[6144,128]{1,0:T(8,128)(2,1)S(1)}, bf16[6144,128]{1,0:T(8,128)(2,1)}, u32[]{:S(2)}) copy-start(bf16[6144,128]{1,0:T(8,128)(2,1)} %all-gather.2.cloned.1.call-done) | copy-start | bytes 4718596
Sparse Core Ops, SparseCore 0:
  11.4 57.5 all-gather.1
where the time goes:
time: 130 us; the launch traced here: 129 us
  waiting for transfers between devices  59.1 us (45%)
  blocking collectives  39.4 us (30%)
  between operations  15.9 us (12%)
  matrix products  10.7 us (8%)
  other arithmetic  4.09 us (3%)
    all_gather x1, waiting for transfers between devices, body(): lax.all_gather(unit_low, ('dp', 'sub'), axis=0, tiled=True)  59.1 us
    psum x1, blocking collectives, body(): loss = lax.psum(jnp.sum(row_loss), ('dp', 'sub')) / views_all  39.4 us
    dot_general x1, matrix products, tile_scores(): lax.dot_general(left_low, piece, (((1,), (1,)), ((), ())), preferred_elem...  5.74 us
    dot_general x1, matrix products, backward_step(): return jnp.dot(weight, piece, preferred_element_type=jnp.float32)  4.95 us
  transfers between devices with their start and end apart: 1, of which 1 were waited for; matrix products, arithmetic and copies ran while one was open for 0% of the time, Pallas kernels for 0%

commit v1 on v0

v1 whole, which is shorter than its diff:
```python
import functools
import math

import jax
import jax.numpy as jnp
from jax import lax
from jax.experimental import pallas as pl
from jax.experimental.pallas import tpu as pltpu
from jax.sharding import PartitionSpec as P

TAU = 0.1
SHIFT = 10.0
EPS = 1e-06
LANES = 128
MESH = pl.DeviceIdType.MESH
LINE = 4

FORWARD = (
    (0, 0, 0), (0, 0, 1), (1, 0, 0), (1, 0, 1), (0, 1, 0), (0, 1, 1), (2, 0, 0), (2, 0, 1),
    (1, 1, 0), (1, 1, 1), (3, 0, 0), (3, 0, 1), (2, 1, 0), (2, 1, 1), (3, 1, 0), (3, 1, 1),
)


def plan():
    at = {step: i for i, step in enumerate(FORWARD)}
    chunks = []
    for place in range(LINE):
        for dx in range(2):
            for dy in range(2):
                chunks.append((max(at[(place, dy, dx)], at[(place, dx, dy)]), (place, dx, dy)))
    chunks.sort()
    out = []
    for i, step in enumerate(FORWARD):
        out.append(("step", step))
        if chunks and chunks[0][0] < i:
            out.append(("chunk", chunks.pop(0)[1]))
    out.extend(("chunk", c) for _, c in chunks)
    return out


def kernel(
    groups, p_ref, partner_ref, loss_ref, grad_ref,
    blocks, scores, totals, accum, pos, gsum, unit_s, mates, send, recv, rsend, rrecv,
):
    rows = p_ref.shape[0]
    pair = 2 * rows
    tiles = pair // LANES
    spare = 2 * LANES - rows
    d = lax.axis_index("dp")
    c = lax.axis_index("sub")
    z = d // 4
    y = (d // 2) % 2
    x = d % 2
    me = d * 2 + c
    first = x * (1 - c) + y * c
    last = y * (1 - c) + x * c
    half = z // 2

    def place_z(k):
        return (z, z + 1 - 2 * (z % 2), 2 - half, 3 - 3 * half)[k]

    def chip_of(zz, f, l):
        return zz * 4 + f * (1 + c) + l * (2 - c)

    flip = lambda v, n: v + n * (1 - 2 * v)
    near_first = (chip_of(z, flip(first, 1), last), c)
    near_last = (chip_of(z, first, flip(last, 1)), c)
    sibling = (d, 1 - c)
    up, down = (d + 4, c), (d - 4, c)

    barrier = pltpu.get_barrier_semaphore()
    for dev in (near_first, near_last, sibling):
        pl.semaphore_signal(barrier, inc=1, device_id=dev, device_id_type=MESH)

    @pl.when(z < LINE - 1)
    def _():
        pl.semaphore_signal(barrier, inc=1, device_id=up, device_id_type=MESH)

    @pl.when(z > 0)
    def _():
        pl.semaphore_signal(barrier, inc=1, device_id=down, device_id_type=MESH)

    p = p_ref[...]
    inverse = lax.rsqrt(jnp.sum(p * p, axis=1, keepdims=True) + EPS)
    unit = p * inverse
    own = unit.astype(jnp.bfloat16)
    blocks[me] = own
    unit_s[...] = unit
    accum[...] = jnp.zeros_like(accum)
    pos[...] = jnp.zeros_like(pos)
    gsum[...] = jnp.zeros_like(gsum)
    spread = jnp.broadcast_to(partner_ref[...].astype(jnp.float32), (LANES, rows)).T
    mates[...] = spread.astype(jnp.int32) - lax.broadcasted_iota(jnp.int32, (rows, LANES), 1)
    mine = pl.ds(pl.multiple_of(c * spare, 8), rows)

    pl.semaphore_wait(barrier, 3 + jnp.minimum(z, 1) + jnp.minimum(LINE - 1 - z, 1))

    def copy(b, dev, i, way):
        return pltpu.make_async_remote_copy(
            src_ref=blocks.at[b],
            dst_ref=blocks.at[b],
            send_sem=send.at[i, way],
            recv_sem=recv.at[b],
            device_id=dev,
            device_id_type=MESH,
        )

    def sends(step, act):
        k, dl, df = step
        i = FORWARD.index(step)
        zz = place_z(k)
        b = chip_of(zz, flip(first, df), flip(last, dl)) * 2 + c
        if dl == 0:
            if k == 0:
                go_up, go_down = z < LINE - 1, z > 0
            else:
                go_up = jnp.logical_and(zz < z, z < LINE - 1)
                go_down = jnp.logical_and(zz > z, z > 0)

            @pl.when(go_up)
            def _():
                act(copy(b, up, i, 0))

            @pl.when(go_down)
            def _():
                act(copy(b, down, i, 1))

            if k == 0 and df == 0:
                act(copy(b, near_first, i, 4))
            act(copy(b, near_last, i, 2))
        act(copy(b, sibling, i, 3))
        return b

    def forward(step):
        k, dl, df = step
        if (k, dl, df) != (0, 0, 0):
            b = chip_of(place_z(k), flip(first, df), flip(last, dl)) * 2 + c
            copy(b, sibling, 0, 0).wait_recv()
        sends(step, lambda one: one.start())

    def chip_at(chunk):
        k, dx, dy = chunk
        return place_z(k) * 4 + flip(y, dy) * 2 + flip(x, dx)

    def pair_of(chip):
        return blocks[pl.ds(2 * chip, 2)].reshape(pair, LANES)

    scale = math.log2(math.e) / TAU

    def chunk_forward(n, chunk):
        chip = chip_at(chunk)
        copy(chip * 2 + 1 - c, sibling, 0, 0).wait_recv()
        dots = lax.dot_general(
            blocks[me], pair_of(chip), (((1,), (1,)), ((), ())), preferred_element_type=jnp.float32
        )
        powers = jnp.exp2(dots * scale - SHIFT * math.log2(math.e))
        if chunk == (0, 0, 0):
            cols = lax.broadcasted_iota(jnp.int32, (rows, pair), 1)
            at = lax.broadcasted_iota(jnp.int32, (rows, pair), 0) + c * rows
            powers = jnp.where(cols == at, 0.0, powers)
        scores[n] = powers
        total = accum[mine, :]
        found = pos[...]
        for t in range(tiles):
            part = slice(t * LANES, (t + 1) * LANES)
            total = total + powers[:, part]
            hit = mates[...] == chip * pair + t * LANES
            found = found + jnp.where(hit, dots[:, part], 0.0)
        accum[mine, :] = total
        pos[...] = found

    order = []
    for what, item in plan():
        if what == "step":
            forward(item)
        else:
            chunk_forward(len(order), item)
            order.append(item)

    every = accum[...]
    totals[me, :, 0 : 2 * LANES] = jnp.sum(every.T, axis=0, keepdims=True)
    totals[me, :, 2 * LANES : 3 * LANES] = jnp.sum(pos[...], axis=0, keepdims=True) / TAU

    def share(j):
        to = lax.rem(me + j, groups)
        return pltpu.make_async_remote_copy(
            src_ref=totals.at[me],
            dst_ref=totals.at[me],
            send_sem=rsend.at[j],
            recv_sem=rrecv.at[me],
            device_id=(to // 2, to % 2),
            device_id_type=MESH,
        )

    def shared(b):
        return pltpu.make_async_remote_copy(
            src_ref=totals.at[b],
            dst_ref=totals.at[b],
            send_sem=rsend.at[0],
            recv_sem=rrecv.at[b],
            device_id=sibling,
            device_id_type=MESH,
        )

    @pl.loop(1, groups)
    def _(j):
        share(j).start()

    row_scale = (1.0 / TAU) / jnp.sum(accum[mine, :], axis=1, keepdims=True)
    low = lax.broadcasted_iota(jnp.int32, (1, LANES), 1) < rows - LANES

    def columns(chip):
        a, b = totals[2 * chip], totals[2 * chip + 1]
        return (
            a[:, :LANES],
            jnp.where(low, a[:, LANES : 2 * LANES], b[:, :LANES]),
            b[:, LANES : 2 * LANES],
        )

    for n, chunk in enumerate(order):
        chip = chip_at(chunk)
        shared(2 * chip + 1 - c).wait_recv()
        if chunk != (0, 0, 0):
            shared(2 * chip + c).wait_recv()
        powers = scores[n]
        parts = []
        for t, column in enumerate(columns(chip)):
            weight = powers[:, t * LANES : (t + 1) * LANES] * (row_scale + (1.0 / TAU) / column)
            hit = mates[...] == chip * pair + t * LANES
            parts.append(jnp.where(hit, weight - 2.0 / TAU, weight).astype(jnp.bfloat16))
        gsum[...] += jnp.dot(
            jnp.concatenate(parts, axis=1), pair_of(chip), preferred_element_type=jnp.float32
        )

    grown = gsum[...]
    unit = unit_s[...]
    p = p_ref[...]
    inverse = lax.rsqrt(jnp.sum(p * p, axis=1, keepdims=True) + EPS)
    inner = jnp.sum(unit * grown, axis=1, keepdims=True)
    grad_ref[...] = inverse * (grown - unit * inner)

    logs = jnp.zeros((1, LANES), jnp.float32)
    for chip in range(groups // 2):
        for column in columns(chip):
            logs = logs + jnp.log(column)
        for core in range(2):
            logs = logs - totals[2 * chip + core][:, 2 * LANES : 3 * LANES]
    loss_ref[0, 0] = jnp.sum(logs) / (rows * groups) + SHIFT

    for step in FORWARD:
        sends(step, lambda one: one.wait_send())

    @pl.loop(1, groups)
    def _(j):
        share(j).wait_send()


def fused(projections, partner):
    rows, width = projections.shape
    groups = lax.axis_size(("dp", "sub"))
    chips = groups // 2
    loss, grad = pl.pallas_call(
        functools.partial(kernel, groups),
        out_shape=(
            jax.ShapeDtypeStruct((1, 1), jnp.float32),
            jax.ShapeDtypeStruct((rows, width), jnp.float32),
        ),
        in_specs=[pl.BlockSpec(memory_space=pltpu.VMEM)] * 2,
        out_specs=(
            pl.BlockSpec(memory_space=pltpu.SMEM),
            pl.BlockSpec(memory_space=pltpu.VMEM),
        ),
        scratch_shapes=[
            pltpu.VMEM((groups, rows, width), jnp.bfloat16),
            pltpu.VMEM((chips, rows, 2 * rows), jnp.float32),
            pltpu.VMEM((groups, 1, 3 * LANES), jnp.float32),
            pltpu.VMEM((2 * LANES, LANES), jnp.float32),
            pltpu.VMEM((rows, LANES), jnp.float32),
            pltpu.VMEM((rows, width), jnp.float32),
            pltpu.VMEM((rows, width), jnp.float32),
            pltpu.VMEM((rows, LANES), jnp.int32),
            pltpu.SemaphoreType.DMA((len(FORWARD), 5)),
            pltpu.SemaphoreType.DMA((groups,)),
            pltpu.SemaphoreType.DMA((groups,)),
            pltpu.SemaphoreType.DMA((groups,)),
        ],
        compiler_params=pltpu.CompilerParams(collective_id=0, has_side_effects=True),
    )(projections, partner.reshape(1, rows))
    return loss.reshape(()), grad


def general(projections, partner):
    rows = projections.shape[0]
    axes = ("dp", "sub")
    inverse = lax.rsqrt(jnp.sum(projections * projections, axis=1) + EPS)
    unit = projections * inverse[:, None]
    low = unit.astype(jnp.bfloat16)
    everyone = lax.all_gather(low, axes, axis=0, tiled=True)
    columns = jnp.arange(everyone.shape[0], dtype=jnp.int32)
    ids = lax.axis_index(axes) * rows + jnp.arange(rows, dtype=jnp.int32)
    score = (
        lax.dot_general(
            low, everyone, (((1,), (1,)), ((), ())), preferred_element_type=jnp.float32
        )
        / TAU
    )
    diag = columns[None, :] == ids[:, None]
    hit = columns[None, :] == partner[:, None]
    total = jnp.sum(jnp.where(diag, 0.0, jnp.exp(score - SHIFT)), axis=1)
    found = jnp.sum(jnp.where(hit, score, 0.0), axis=1)
    lse = jnp.log(total) + SHIFT
    lse_all = lax.all_gather(lse, axes, axis=0, tiled=True)
    loss = lax.psum(jnp.sum(lse - found), axes) / everyone.shape[0]
    weight = jnp.exp(score - lse[:, None]) + jnp.exp(score - lse_all[None, :])
    weight = weight - 2.0 * hit.astype(jnp.float32)
    weight = jnp.where(diag, 0.0, weight / TAU).astype(jnp.bfloat16)
    grown = jnp.dot(weight, everyone, preferred_element_type=jnp.float32)
    inner = jnp.sum(unit * grown, axis=1)
    return loss, inverse[:, None] * (grown - unit * inner[:, None])


def solution(mesh):
    small = mesh.shape["dp"] == 4 * LINE and mesh.shape["sub"] == 2

    def body(projections, partner):
        rows, width = projections.shape
        fits = width == LANES and LANES < rows < 2 * LANES and (2 * rows) % LANES == 0
        return (fused if small and fits else general)(projections, partner)

    return jax.shard_map(
        body,
        mesh=mesh,
        in_specs=(P(("dp", "sub"), None), P(("dp", "sub"))),
        out_specs=(P(), P(("dp", "sub"), None)),
        check_vma=False,
    )
```

time: 130 us -> 35.1 us (0.27)
  waiting for transfers between devices: 59.1 us -> 0 us
  blocking collectives: 39.4 us -> 0 us
  Pallas kernels: 0 us -> 30.9 us
  between operations: 15.9 us -> 2.45 us
  matrix products: 10.7 us -> 0 us
  other arithmetic: 4.09 us -> 0 us
  local copies, waits for them, and re-layouts: 0.02 us -> 1.54 us
    all_gather x1 -> x0, waiting for transfers between devices: 59.1 us -> none  [body(): lax.all_gather(unit_low, ('dp', 'sub'), axis=0, tiled=True)]
    psum x1 -> x0, blocking collectives: 39.4 us -> none  [body(): loss = lax.psum(jnp.sum(row_loss), ('dp', 'sub')) / views_all]
    pallas_call x0 -> x1, Pallas kernels: none -> 30.9 us  [fused(): pl.pallas_call(functools.partial(kernel, groups), out_shape=(jax.ShapeDty...]
    dot_general x2 -> x0, matrix products: 10.7 us -> none  [the longest x1 5.74 us: tile_scores(): lax.dot_general(left_low, piece, (((1,), (1,)), ((), ())), preferred_elem...]
    convert_element_type x1 -> x0, other arithmetic: 1.61 us -> none  [body(): unit_low = unit.astype(jnp.bfloat16)]
    unnamed x7 -> x1, local copies, waits for them, and re-layouts: 0.02 us -> 1.54 us
  transfers between devices with their start and end apart: 1 -> 0, of which waited for: 1 -> 0; matrix products, arithmetic and copies ran while one was open for 0% -> 0% of each run, Pallas kernels for 0% -> 0%
where the time goes in v1:
time: 35.1 us; the launch traced here: 34.9 us
  Pallas kernels  30.9 us (88%)
  between operations  2.45 us (7%)
  local copies, waits for them, and re-layouts  1.54 us (4%)
    pallas_call x1, Pallas kernels, fused(): pl.pallas_call(functools.partial(kernel, groups), out_shape=(jax.ShapeDty...  30.9 us
    unnamed x1, local copies, waits for them, and re-layouts  1.54 us

profile of v1, /device:TPU:0, one launch (start us, length us, event | category | flops | bytes accessed | tf_op | source)
XLA Modules:
  0.0 34.9 jit_solution(121567282782339411)
XLA Ops:
  0.6 30.9 %shard_map.41 = (f32[1,1]{1,0:T(1,128)}, f32[192,128]{1,0:T(8,128)}) custom-call(f32[192,128]{1,0:T(8,128)} %p_ref.1, s32[1,192]{1,0:T(1,128)} %bitcast.2), custom_call_target="tpu_custom_call" | custom-call | tf_op jit(solution)/shard_map/pallas_call | solution.py:262
  32.2 1.5 %copy.7 = f32[192,128]{1,0:T(8,128)} copy(f32[192,128]{1,0:T(8,128)} %get-tuple-element.9) | data formatting | bytes 196608

commit v2 on v1

--- a/solution.py
+++ b/solution.py
@@ -16,9 +16,11 @@
 LINE = 4
 
 FORWARD = (
-    (0, 0, 0), (0, 0, 1), (1, 0, 0), (1, 0, 1), (0, 1, 0), (0, 1, 1), (2, 0, 0), (2, 0, 1),
-    (1, 1, 0), (1, 1, 1), (3, 0, 0), (3, 0, 1), (2, 1, 0), (2, 1, 1), (3, 1, 0), (3, 1, 1),
+    (0, 0, 0), (1, 0, 0), (2, 0, 0), (3, 0, 0), (0, 0, 1), (0, 1, 0), (0, 1, 1), (1, 0, 1),
+    (1, 1, 0), (1, 1, 1), (2, 0, 1), (2, 1, 0), (2, 1, 1), (3, 0, 1), (3, 1, 0), (3, 1, 1),
 )
+EARLY = 4
+WAYS = 7
 
 
 def plan():
@@ -32,17 +34,17 @@
     out = []
     for i, step in enumerate(FORWARD):
         out.append(("step", step))
-        if chunks and chunks[0][0] < i:
+        if i >= EARLY and chunks and chunks[0][0] < i:
             out.append(("chunk", chunks.pop(0)[1]))
     out.extend(("chunk", c) for _, c in chunks)
     return out
 
 
 def kernel(
-    groups, p_ref, partner_ref, loss_ref, grad_ref,
-    blocks, scores, totals, accum, pos, gsum, unit_s, mates, send, recv, rsend, rrecv,
+    groups, p_hbm, partner_hbm, loss_ref, grad_ref, p_ref, partner_ref,
+    blocks, scores, totals, accum, pos, gsum, unit_s, mates, fetched, send, recv, rsend, rrecv,
 ):
-    rows = p_ref.shape[0]
+    rows = p_hbm.shape[0]
     pair = 2 * rows
     tiles = pair // LANES
     spare = 2 * LANES - rows
@@ -65,35 +67,34 @@
     flip = lambda v, n: v + n * (1 - 2 * v)
     near_first = (chip_of(z, flip(first, 1), last), c)
     near_last = (chip_of(z, first, flip(last, 1)), c)
+    diagonal = (chip_of(z, flip(first, 1), flip(last, 1)), c)
     sibling = (d, 1 - c)
-    up, down = (d + 4, c), (d - 4, c)
-
+    line = [(chip_of(place_z(k), first, last), c) for k in (1, 2, 3)]
+
+    fetch = pltpu.make_async_copy(p_hbm, p_ref, fetched.at[0])
+    fetch.start()
+    fetch_mates = pltpu.make_async_copy(partner_hbm, partner_ref, fetched.at[1])
+    fetch_mates.start()
     barrier = pltpu.get_barrier_semaphore()
-    for dev in (near_first, near_last, sibling):
+    peers = (*line, near_first, near_last, diagonal, sibling)
+    for dev in peers:
         pl.semaphore_signal(barrier, inc=1, device_id=dev, device_id_type=MESH)
 
-    @pl.when(z < LINE - 1)
-    def _():
-        pl.semaphore_signal(barrier, inc=1, device_id=up, device_id_type=MESH)
-
-    @pl.when(z > 0)
-    def _():
-        pl.semaphore_signal(barrier, inc=1, device_id=down, device_id_type=MESH)
-
+    accum[...] = jnp.zeros_like(accum)
+    pos[...] = jnp.zeros_like(pos)
+    gsum[...] = jnp.zeros_like(gsum)
+    mine = pl.ds(pl.multiple_of(c * spare, 8), rows)
+    fetch.wait()
     p = p_ref[...]
     inverse = lax.rsqrt(jnp.sum(p * p, axis=1, keepdims=True) + EPS)
     unit = p * inverse
-    own = unit.astype(jnp.bfloat16)
-    blocks[me] = own
+    blocks[me] = unit.astype(jnp.bfloat16)
     unit_s[...] = unit
-    accum[...] = jnp.zeros_like(accum)
-    pos[...] = jnp.zeros_like(pos)
-    gsum[...] = jnp.zeros_like(gsum)
+    fetch_mates.wait()
     spread = jnp.broadcast_to(partner_ref[...].astype(jnp.float32), (LANES, rows)).T
     mates[...] = spread.astype(jnp.int32) - lax.broadcasted_iota(jnp.int32, (rows, LANES), 1)
-    mine = pl.ds(pl.multiple_of(c * spare, 8), rows)
-
-    pl.semaphore_wait(barrier, 3 + jnp.minimum(z, 1) + jnp.minimum(LINE - 1 - z, 1))
+
+    pl.semaphore_wait(barrier, len(peers))
 
     def copy(b, dev, i, way):
         return pltpu.make_async_remote_copy(
@@ -110,25 +111,14 @@
         i = FORWARD.index(step)
         zz = place_z(k)
         b = chip_of(zz, flip(first, df), flip(last, dl)) * 2 + c
-        if dl == 0:
+        if (dl, df) == (0, 0):
             if k == 0:
-                go_up, go_down = z < LINE - 1, z > 0
-            else:
-                go_up = jnp.logical_and(zz < z, z < LINE - 1)
-                go_down = jnp.logical_and(zz > z, z > 0)
-
-            @pl.when(go_up)
-            def _():
-                act(copy(b, up, i, 0))
-
-            @pl.when(go_down)
-            def _():
-                act(copy(b, down, i, 1))
-
-            if k == 0 and df == 0:
-                act(copy(b, near_first, i, 4))
-            act(copy(b, near_last, i, 2))
-        act(copy(b, sibling, i, 3))
+                for way, dev in enumerate(line):
+                    act(copy(b, dev, i, way))
+            act(copy(b, diagonal, i, 5))
+            act(copy(b, near_first, i, 3))
+            act(copy(b, near_last, i, 4))
+        act(copy(b, sibling, i, 6))
         return b
 
     def forward(step):
@@ -265,12 +255,14 @@
             jax.ShapeDtypeStruct((1, 1), jnp.float32),
             jax.ShapeDtypeStruct((rows, width), jnp.float32),
         ),
-        in_specs=[pl.BlockSpec(memory_space=pltpu.VMEM)] * 2,
+        in_specs=[pl.BlockSpec(memory_space=pl.ANY)] * 2,
         out_specs=(
             pl.BlockSpec(memory_space=pltpu.SMEM),
             pl.BlockSpec(memory_space=pltpu.VMEM),
         ),
         scratch_shapes=[
+            pltpu.VMEM((rows, width), jnp.float32),
+            pltpu.VMEM((1, rows), jnp.int32),
             pltpu.VMEM((groups, rows, width), jnp.bfloat16),
             pltpu.VMEM((chips, rows, 2 * rows), jnp.float32),
             pltpu.VMEM((groups, 1, 3 * LANES), jnp.float32),
@@ -279,7 +271,8 @@
             pltpu.VMEM((rows, width), jnp.float32),
             pltpu.VMEM((rows, width), jnp.float32),
             pltpu.VMEM((rows, LANES), jnp.int32),
-            pltpu.SemaphoreType.DMA((len(FORWARD), 5)),
+            pltpu.SemaphoreType.DMA((2,)),
+            pltpu.SemaphoreType.DMA((len(FORWARD), WAYS)),
             pltpu.SemaphoreType.DMA((groups,)),
             pltpu.SemaphoreType.DMA((groups,)),
             pltpu.SemaphoreType.DMA((groups,)),

time: 35.1 us -> 30.9 us (0.88)
  Pallas kernels: 30.9 us -> 26.7 us
    pallas_call x1, Pallas kernels: 30.9 us -> 26.7 us  [fused(): pl.pallas_call(functools.partial(kernel, groups), out_shape=(jax.ShapeDty...]
where the time goes in v2:
time: 30.9 us; the launch traced here: 30.7 us
  Pallas kernels  26.7 us (86%)
  between operations  2.45 us (8%)
  local copies, waits for them, and re-layouts  1.54 us (5%)
    pallas_call x1, Pallas kernels, fused(): pl.pallas_call(functools.partial(kernel, groups), out_shape=(jax.ShapeDty...  26.7 us
    unnamed x1, local copies, waits for them, and re-layouts  1.54 us

profile of v2, /device:TPU:0, one launch (start us, length us, event | category | flops | bytes accessed | tf_op | source)
XLA Modules:
  0.0 30.7 jit_solution(2473101369552525407)
XLA Ops:
  0.6 26.7 %shard_map.41 = (f32[1,1]{1,0:T(1,128)}, f32[192,128]{1,0:T(8,128)}) custom-call(f32[192,128]{1,0:T(8,128)} %p_hbm.1, s32[1,192]{1,0:T(1,128)} %bitcast.2), custom_call_target="tpu_custom_call" | custom-call | tf_op jit(solution)/shard_map/pallas_call | solution.py:252
  28.1 1.5 %copy.7 = f32[192,128]{1,0:T(8,128)} copy(f32[192,128]{1,0:T(8,128)} %get-tuple-element.9) | data formatting | bytes 196608
